TPU v7x, 32 devices: a whole 2x2x4 slice. The times are simulated.
32 devices in a mesh: dp: 8 (over z, y), mp: 4 (over x, core).
Axes of the slice: x: 2, y: 2, z: 4, core: 2. Of those that a mesh axis runs over, the one named last changes fastest.
Arguments:
- slow_weights: float32 [1, 3584, 1024], P(None, None, 'mp'), may hold values from -6 to 6
- fast_weights: bfloat16 [8, 1, 3584, 1024], P('dp', None, None, 'mp'), may hold values from -64 to 64
- momentum: float32 [1, 3584, 1024], P(None, None, 'mp'), may hold values from -1.2 to 1.2
Outputs:
- slow_next: float32 [1, 3584, 1024], P(None, None, 'mp')
- momentum_next: float32 [1, 3584, 1024], P(None, None, 'mp')
- fast_next: bfloat16 [8, 1, 3584, 1024], P('dp', None, None, 'mp')
All inputs are finite; a program needn't handle non-finite values.
Results may differ from a plain program's by a relative error of at most 0.001.
Values sent between devices are 32-bit elements; how exact they have to be, the bound alone decides.
A program may use at most 64 MiB of HBM per device.

v0:
```python
import math
import jax
import jax.numpy as jnp
from jax import lax
from jax.sharding import PartitionSpec as P

MOMENTUM_RATE = 0.9
OUTER_RATE = 0.7
CLIP_LEVEL = 0.2
EPSILON = 1e-06


def apply_update(slow_part, momentum_part, pseudo, squares, max_norm):
    factor = jnp.minimum(1.0, max_norm / (jnp.sqrt(squares) + EPSILON))
    gradient = factor * pseudo
    momentum_next = MOMENTUM_RATE * momentum_part + gradient
    slow_next = slow_part - OUTER_RATE * (gradient + MOMENTUM_RATE * momentum_next)
    return (slow_next, momentum_next)


def body(slow_weights, fast_weights, momentum):
    difference = slow_weights - fast_weights[0].astype(jnp.float32)
    replicas = lax.axis_size("dp")
    entries = (
        slow_weights.shape[0] * slow_weights.shape[1] * slow_weights.shape[2] * lax.axis_size("mp")
    )
    max_norm = CLIP_LEVEL * math.sqrt(entries)
    pseudo = lax.psum(difference, "dp") / replicas
    squares = lax.psum(jnp.sum(pseudo * pseudo), "mp")
    slow_next, momentum_next = apply_update(slow_weights, momentum, pseudo, squares, max_norm)
    fast_next = slow_next.astype(jnp.bfloat16)[None]
    return (slow_next, momentum_next, fast_next)


def solution(mesh):
    in_specs = (P(None, None, "mp"), P("dp", None, None, "mp"), P(None, None, "mp"))
    out_specs = (P(None, None, "mp"), P(None, None, "mp"), P("dp", None, None, "mp"))
    return jax.shard_map(body, mesh=mesh, in_specs=in_specs, out_specs=out_specs, check_vma=False)
```

profile of v0, /device:TPU:0, one launch (start us, length us, event | category | flops | bytes accessed | tf_op | source)
XLA Modules:
  0.0 184.9 jit_solution(11704129445931743159)
XLA Ops:
  7.2 0.0 all-reduce.2.cloned.1.call-start
  7.2 4.8 %convert_subtract_fusion = f32[1,3584,256]{2,1,0:T(8,128)} fusion(f32[1,3584,256]{2,1,0:T(8,128)} %param.3, bf16[1,1,3584,256]{3,2,1,0:T(8,128)(2,1)} %param.4), kind=kLoop, calls=%fused_computation | loop fusion | flops 1835008 | bytes 9175040 | tf_op jit(solution)/shard_map/sub | solution.py:22
  12.0 0.0 all-reduce.2.cloned.1.call-update
  12.0 145.8 %all-reduce.2.cloned.1.call-done = f32[1,3584,256]{2,1,0:T(8,128)} async-done(((f32[1,3584,256]{2,1,0:T(8,128)}), f32[1,3584,256]{2,1,0:T(8,128)}) %all-reduce.2.cloned.1.call-update) | async-done | bytes 3670032 | tf_op jit(solution)/shard_map/psum | solution.py:28
  157.8 3.6 %multiply_reduce_fusion = f32[]{:T(128)} fusion(f32[1,3584,256]{2,1,0:T(8,128)} %all-reduce.2.cloned.1.call-done), kind=kLoop, calls=%fused_computation.3 | loop fusion | flops 2752511 | bytes 3670020 | tf_op jit(solution)/shard_map/reduce_sum | solution.py:29
  161.4 7.0 %psum.15 = f32[]{:T(128)} all-reduce(f32[]{:T(128)} %multiply_reduce_fusion), channel_id=1, replica_groups=mesh['dp'=8,'mp'=4] {'mp'}, use_global_device_ids=true, to_apply=%region_2.0 | all-reduce | flops 1 | bytes 8 | tf_op jit(solution)/shard_map/psum | solution.py:29
  169.2 8.9 %convert_bitcast_fusion = (bf16[1,1,3584,256]{3,2,1,0:T(8,128)(2,1)}, f32[1,3584,256]{2,1,0:T(8,128)}, f32[1,3584,256]{2,1,0:T(8,128)}) fusion(f32[1,3584,256]{2,1,0:T(8,128)} %param.3, f32[1,3584,256]{2,1,0:T(8,128)} %all-reduce.2.cloned.1.call-done, f32[]{:T(128)S(6)} %mul.24, f32[1,3584,256]{2,1,0:T(8,128)} %param.5), kind=kLoop, calls=%fused_computation.4 | loop fusion | flops 7340032 | bytes 20185092 | tf_op jit(solution)/shard_map/broadcast_in_dim | solution.py:31
Async XLA Ops:
  7.2 150.7 %all-reduce.2.cloned.1.call-start = ((), (), s32[]{:S(2)}) async-start(), calls=%async_computation | async-start | bytes 7340032 | tf_op jit(solution)/shard_map/psum | solution.py:28
Sparse Core Ops, SparseCore 0:
  12.2 145.5 all-reduce.1
where the time goes:
time: 185 us
  waiting for transfers between devices  146 us (79%)
  other arithmetic  17.3 us (9%)
  between operations  14.8 us (8%)
  blocking collectives  7 us (4%)
    psum x1, waiting for transfers between devices, body(): pseudo = lax.psum(difference, 'dp') / replicas  146 us
    broadcast_in_dim x1, other arithmetic, body(): fast_next = slow_next.astype(jnp.bfloat16)[None]  8.86 us
    psum x1, blocking collectives, body(): squares = lax.psum(jnp.sum(pseudo * pseudo), 'mp')  7 us
    sub x1, other arithmetic, body(): difference = slow_weights - fast_weights[0].astype(jnp.float32)  4.8 us
  transfers between devices with their start and end apart: 1, of which 1 were waited for; matrix products, arithmetic and copies ran while one was open for 0% of the time, Pallas kernels for 0%

commit v1 on v0

--- a/solution.py
+++ b/solution.py
@@ -25,7 +25,7 @@
         slow_weights.shape[0] * slow_weights.shape[1] * slow_weights.shape[2] * lax.axis_size("mp")
     )
     max_norm = CLIP_LEVEL * math.sqrt(entries)
-    pseudo = lax.psum(difference, "dp") / replicas
+    pseudo = jnp.sum(lax.all_gather(difference, "dp"), axis=0) / replicas
     squares = lax.psum(jnp.sum(pseudo * pseudo), "mp")
     slow_next, momentum_next = apply_update(slow_weights, momentum, pseudo, squares, max_norm)
     fast_next = slow_next.astype(jnp.bfloat16)[None]

time: 185 us -> 614 us (3.32)
  waiting for transfers between devices: 146 us -> 562 us
  other arithmetic: 17.3 us -> 30.1 us
    all_gather x0 -> x1, waiting for transfers between devices: none -> 562 us  [body(): pseudo = jnp.sum(lax.all_gather(difference, 'dp'), axis=0) / replicas]
    psum x1 -> x0, waiting for transfers between devices: 146 us -> none  [body(): pseudo = lax.psum(difference, 'dp') / replicas]
    reduce_sum x0 -> x1, other arithmetic: none -> 12.8 us  [body(): pseudo = jnp.sum(lax.all_gather(difference, 'dp'), axis=0) / replicas]
where the time goes in v1:
time: 614 us
  waiting for transfers between devices  562 us (92%)
  other arithmetic  30.1 us (5%)
  between operations  14.8 us (2%)
  blocking collectives  7 us (1%)
    all_gather x1, waiting for transfers between devices, body(): pseudo = jnp.sum(lax.all_gather(difference, 'dp'), axis=0) / replicas  562 us
    reduce_sum x1, other arithmetic, body(): pseudo = jnp.sum(lax.all_gather(difference, 'dp'), axis=0) / replicas  12.8 us
  transfers between devices with their start and end apart: 1, of which 1 were waited for; matrix products, arithmetic and copies ran while one was open for 0% of the time, Pallas kernels for 0%

profile of v1, /device:TPU:0, one launch (start us, length us, event | category | flops | bytes accessed | tf_op | source)
XLA Modules:
  0.0 613.8 jit_solution(15679763960862142895)
XLA Ops:
  7.2 0.0 all-gather.3.cloned.1.call-start
  7.2 4.8 convert_subtract_fusion
  12.0 0.0 all-gather.3.cloned.1.call-update
  12.0 561.9 %all-gather.3.cloned.1.call-done = f32[8,3584,256]{2,1,0:T(8,128)} async-done(((f32[1,3584,256]{2,1,0:T(8,128)}), f32[8,3584,256]{2,1,0:T(8,128)}) %all-gather.3.cloned.1.call-update) | async-done | bytes 29360144 | tf_op jit(solution)/shard_map/all_gather | solution.py:28
  573.9 12.8 %reduce.2 = f32[3584,256]{1,0:T(8,128)} reduce(f32[8,3584,256]{2,1,0:T(8,128)} %all-gather.3.cloned.1.call-done, f32[]{:T(128)} %constant.1.clone.1), dimensions={0}, to_apply=%region_0.0 | reduce | flops 6422528 | bytes 33030148 | tf_op jit(solution)/shard_map/reduce_sum | solution.py:28
  586.7 3.6 multiply_reduce_fusion
  590.3 7.0 %psum.7 = f32[]{:T(128)} all-reduce(f32[]{:T(128)} %multiply_reduce_fusion), channel_id=1, replica_groups=mesh['dp'=8,'mp'=4] {'mp'}, use_global_device_ids=true, to_apply=%region_2.0 | all-reduce | flops 1 | bytes 8 | tf_op jit(solution)/shard_map/psum | solution.py:29
  598.1 8.9 %convert_bitcast_fusion = (bf16[1,1,3584,256]{3,2,1,0:T(8,128)(2,1)}, f32[1,3584,256]{2,1,0:T(8,128)}, f32[1,3584,256]{2,1,0:T(8,128)}) fusion(f32[1,3584,256]{2,1,0:T(8,128)} %param.3, f32[3584,256]{1,0:T(8,128)} %reduce.2, f32[]{:T(128)S(6)} %mul.40, f32[1,3584,256]{2,1,0:T(8,128)} %param.5), kind=kLoop, calls=%fused_computation.6 | loop fusion | flops 7340032 | bytes 20185092 | tf_op jit(solution)/shard_map/broadcast_in_dim | solution.py:31
Async XLA Ops:
  7.2 566.8 %all-gather.3.cloned.1.call-start = ((), (), s32[]{:S(2)}) async-start(), calls=%async_computation | async-start | bytes 33030144 | tf_op jit(solution)/shard_map/all_gather | solution.py:28
Sparse Core Ops, SparseCore 0:
  12.2 561.7 all-gather.2
